TPU v7x, 32 devices: a whole 2x2x4 slice. The times are simulated.
32 devices in a mesh: rep: 8 (over y, x, core), tp: 4 (over z).
Axes of the slice: x: 2, y: 2, z: 4, core: 2. Of those that a mesh axis runs over, the one named last changes fastest.
Arguments:
- tokens: bfloat16 [8192, 1280], P(('rep', 'tp')), may hold values from -6 to 6
- view_ids: int32 [32, 4], P('rep'), may hold values from 0 to 31
- time_ids: int32 [32], P('rep'), may hold values from 0 to 999
- camera_table: float32 [32, 1280], replicated, may hold values from -6 to 6
- norm_attn: float32 [2, 1280], replicated, may hold values from 0.1 to 1.9
- norm_ffn: float32 [2, 1280], replicated, may hold values from 0.1 to 1.9
- w_query: bfloat16 [2, 1280, 1280], P(None, ('rep', 'tp')), may hold values from -0.1677051 to 0.1677051
- w_key: bfloat16 [2, 1280, 1280], P(None, ('rep', 'tp')), may hold values from -6.764106 to 6.764106
- w_value: bfloat16 [2, 1280, 1280], P(None, ('rep', 'tp')), may hold values from -0.15625 to 0.15625
- w_out: bfloat16 [2, 1280, 1280], P(None, ('rep', 'tp')), may hold values from -0.15625 to 0.15625
- w_gate: bfloat16 [2, 1280, 5120], P(None, ('rep', 'tp')), may hold values from -0.15625 to 0.15625
- w_up: bfloat16 [2, 1280, 5120], P(None, ('rep', 'tp')), may hold values from -0.15625 to 0.15625
- w_down: bfloat16 [2, 1280, 5120], P(None, ('rep', 'tp')), may hold values from -0.078125 to 0.078125
Outputs:
- denoised: bfloat16 [8192, 1280], P(('rep', 'tp'))
All inputs are finite; a program needn't handle non-finite values.
Results may differ from a plain program's by a relative error of at most 0.035.
Values may be sent and summed in bfloat16 or wider, within the bound.
No kernel may reach another device: no remote copies, remote signals or barrier semaphores. Data moves between devices by JAX's collectives and lax.ppermute only.
A program may use at most 128 MiB of HBM per device.

v0:
```python
import math

import jax
import jax.numpy as jnp
from jax import lax
from jax.sharding import PartitionSpec as P

D = 1280
HEADS = 8
VIEWS = 4
HW = 64
LAYERS = 2


def layer_norm(activations, gain_vector):
    average = jnp.mean(activations, axis=-1, keepdims=True)
    centred = activations - average
    spread = jnp.mean(centred * centred, axis=-1, keepdims=True)
    return (centred * lax.rsqrt(spread + 1e-05) * gain_vector).astype(jnp.bfloat16)


def time_code(step_ids, width):
    half_width = width // 2
    frequency = jnp.exp(-math.log(10000.0) * jnp.arange(half_width, dtype=jnp.float32) / half_width)
    angles = step_ids.astype(jnp.float32)[:, None] * frequency[None, :]
    return jnp.concatenate([jnp.cos(angles), jnp.sin(angles)], axis=1)


def conditioning(row_ids, view_ids, time_ids, camera_table):
    set_ids = row_ids // (VIEWS * HW)
    slot_ids = set_ids * VIEWS + row_ids // HW % VIEWS
    flat_views = view_ids.reshape(-1)
    slot_range = jnp.arange(flat_views.shape[0], dtype=jnp.int32)
    pose_ids = jnp.sum(
        jnp.where(slot_ids[:, None] == slot_range[None, :], flat_views[None, :], 0), axis=1
    )
    set_range = jnp.arange(time_ids.shape[0], dtype=jnp.int32)
    step_ids = jnp.sum(
        jnp.where(set_ids[:, None] == set_range[None, :], time_ids[None, :], 0), axis=1
    )
    pose_range = jnp.arange(camera_table.shape[0], dtype=jnp.int32)
    onehot_pose = (pose_ids[:, None] == pose_range[None, :]).astype(jnp.float32)
    camera = jnp.dot(onehot_pose, camera_table, precision=lax.Precision.HIGHEST)
    return camera + time_code(step_ids, camera_table.shape[1])


def reshard(weights):
    owned = (
        lax.all_to_all(weights[0], "tp", split_axis=2, concat_axis=1, tiled=True),
        lax.all_to_all(weights[1], "tp", split_axis=2, concat_axis=1, tiled=True),
        lax.all_to_all(weights[2], "tp", split_axis=2, concat_axis=1, tiled=True),
        lax.all_to_all(weights[3], "tp", split_axis=2, concat_axis=1, tiled=True),
        lax.all_to_all(weights[4], "tp", split_axis=2, concat_axis=1, tiled=True),
        lax.all_to_all(weights[5], "tp", split_axis=2, concat_axis=1, tiled=True),
        lax.all_to_all(weights[6], "tp", split_axis=2, concat_axis=1, tiled=True),
    )
    return (
        lax.all_gather(owned[0], "rep", axis=1, tiled=True),
        lax.all_gather(owned[1], "rep", axis=1, tiled=True),
        lax.all_gather(owned[2], "rep", axis=1, tiled=True),
        lax.all_gather(owned[3], "rep", axis=1, tiled=True),
        lax.all_gather(owned[4], "rep", axis=1, tiled=True),
        lax.all_gather(owned[5], "rep", axis=1, tiled=True),
        lax.all_gather(owned[6], "rep", axis=1, tiled=True),
    )


def attend(packed, width_local, head_size):
    total_rows = packed.shape[0]
    set_count = total_rows // (VIEWS * HW)
    heads_here = width_local // head_size
    shape_heads = (set_count, VIEWS * HW, heads_here, head_size)
    query_rows = packed[:, :width_local].reshape(shape_heads)
    key_rows = packed[:, width_local : 2 * width_local].reshape(shape_heads)
    value_rows = packed[:, 2 * width_local :].reshape(shape_heads)
    scores = jnp.einsum(
        "bqhd,bkhd->bhqk", query_rows, key_rows, preferred_element_type=jnp.float32
    ) * head_size ** (-0.5)
    peak = jnp.max(scores, axis=-1, keepdims=True)
    expons = jnp.exp(scores - peak)
    attn_probs = (expons / jnp.sum(expons, axis=-1, keepdims=True)).astype(jnp.bfloat16)
    mixed_rows = jnp.einsum(
        "bhqk,bkhd->bqhd", attn_probs, value_rows, preferred_element_type=jnp.float32
    )
    return mixed_rows.astype(jnp.bfloat16).reshape(total_rows, width_local)


def out_terms(mixed_rows, weight):
    return lax.dot_general(
        mixed_rows, weight, (((1,), (1,)), ((), ())), preferred_element_type=jnp.float32
    )


def body(
    tokens,
    view_ids,
    time_ids,
    camera_table,
    norm_attn,
    norm_ffn,
    w_query,
    w_key,
    w_value,
    w_out,
    w_gate,
    w_up,
    w_down,
):
    tp_count = lax.axis_size("tp")
    query_w, key_w, value_w, out_w, gate_w, up_w, down_w = reshard(
        (w_query, w_key, w_value, w_out, w_gate, w_up, w_down)
    )
    width_local = query_w.shape[2]
    head_size = D // HEADS
    share_rows = tokens.shape[0]
    group_total = share_rows * tp_count
    first_row = lax.axis_index("tp") * share_rows
    whole_rows = lax.all_gather(tokens, "tp", axis=0, tiled=True)
    row_ids = jnp.arange(group_total, dtype=jnp.int32)
    stream = whole_rows.astype(jnp.float32) + conditioning(
        row_ids, view_ids, time_ids, camera_table
    )

    def total_terms(partial_value):
        return lax.psum(partial_value.astype(jnp.bfloat16), "tp").astype(jnp.float32)

    for layer_index in range(LAYERS):
        query_here = query_w[layer_index]
        key_here = key_w[layer_index]
        value_here = value_w[layer_index]
        gate_here = gate_w[layer_index]
        up_here = up_w[layer_index]
        normed = layer_norm(stream, norm_attn[layer_index])
        packed = jnp.concatenate(
            [
                jnp.dot(normed, query_here, preferred_element_type=jnp.float32).astype(
                    jnp.bfloat16
                ),
                jnp.dot(normed, key_here, preferred_element_type=jnp.float32).astype(jnp.bfloat16),
                jnp.dot(normed, value_here, preferred_element_type=jnp.float32).astype(
                    jnp.bfloat16
                ),
            ],
            axis=1,
        )
        mixed_rows = attend(packed, width_local, head_size)
        stream = stream + total_terms(out_terms(mixed_rows, out_w[layer_index]))
        normed = layer_norm(stream, norm_ffn[layer_index])
        gate_part = jnp.dot(normed, gate_here, preferred_element_type=jnp.float32)
        up_part = jnp.dot(normed, up_here, preferred_element_type=jnp.float32)
        hidden = (jax.nn.gelu(gate_part, approximate=False) * up_part).astype(jnp.bfloat16)
        stream = stream + total_terms(out_terms(hidden, down_w[layer_index]))
    return lax.dynamic_slice_in_dim(stream, first_row, share_rows, 0).astype(jnp.bfloat16)


def solution(mesh):
    return jax.shard_map(
        body,
        mesh=mesh,
        in_specs=(
            P(("rep", "tp"), None),
            P("rep", None),
            P("rep"),
            P(),
            P(),
            P(),
            P(None, ("rep", "tp"), None),
            P(None, ("rep", "tp"), None),
            P(None, ("rep", "tp"), None),
            P(None, ("rep", "tp"), None),
            P(None, ("rep", "tp"), None),
            P(None, ("rep", "tp"), None),
            P(None, ("rep", "tp"), None),
        ),
        out_specs=P(("rep", "tp"), None),
        check_vma=False,
    )
```

profile of v0, /device:TPU:0, one launch (start us, length us, event | category | flops | bytes accessed | tf_op | source)
XLA Modules:
  0.0 892.5 jit_solution(10918619393631502398)
XLA Ops:
  9.8 13.8 %all_to_all.126 = bf16[4,2,12800]{2,1,0:T(2,128)(2,1)S(1)} all-to-all(bf16[4,2,12800]{2,1,0:T(2,128)(2,1)S(1)} %reshape.139), channel_id=1, replica_groups=mesh['rep'=8,'tp'=4] {'tp'}, dimensions={0} | all-to-all | bytes 409600 | tf_op jit(solution)/shard_map/all_to_all | solution.py:49
  27.8 19.7 %all_to_all.127 = bf16[4,2,12800]{2,1,0:T(2,128)(2,1)S(1)} all-to-all(bf16[4,2,12800]{2,1,0:T(2,128)(2,1)S(1)} %reshape.137), channel_id=1, replica_groups=mesh['rep'=8,'tp'=4] {'tp'}, dimensions={0} | all-to-all | bytes 409600 | tf_op jit(solution)/shard_map/all_to_all | solution.py:50
  51.7 14.9 %all_to_all.128 = bf16[4,2,12800]{2,1,0:T(2,128)(2,1)S(1)} all-to-all(bf16[4,2,12800]{2,1,0:T(2,128)(2,1)S(1)} %reshape.141), channel_id=1, replica_groups=mesh['rep'=8,'tp'=4] {'tp'}, dimensions={0} | all-to-all | bytes 409600 | tf_op jit(solution)/shard_map/all_to_all | solution.py:51
  71.3 4.0 all-to-all-start.3
  75.7 10.5 %multiply_cosine_fusion = (f32[1024,640]{1,0:T(8,128)S(1)}, f32[1024,640]{1,0:T(8,128)}) fusion(f32[640]{0:T(1024)S(1)} %multiply_exponential_fusion, f32[1024]{0:T(1024)S(1)} %convert_element_type.93), kind=kLoop, calls=%fused_computation.60 | loop fusion | flops 655360 | bytes 5249536 | tf_op jit(solution)/shard_map/cos | solution.py:26
  91.8 5.1 fusion.139
  100.0 4.8 all-gather.13.cloned.1.call-done
  104.8 3.1 convolution_convert_fusion.10
  109.7 24.3 %all-gather.15.cloned.1.call-done = bf16[2,1280,320]{2,1,0:T(8,128)(2,1)} async-done(((bf16[2,160,320]{2,1,0:T(8,128)(2,1)}), bf16[2,1280,320]{2,1,0:T(8,128)(2,1)}) %all-gather.15.cloned.1.call-update) | async-done | bytes 1638416 | tf_op jit(solution)/shard_map/all_gather | solution.py:59
  133.9 3.1 convolution_convert_fusion.9
  139.5 23.4 %all-gather.11.cloned.1.call-done = bf16[2,1280,320]{2,1,0:T(8,128)(2,1)} async-done(((bf16[2,160,320]{2,1,0:T(8,128)(2,1)}), bf16[2,1280,320]{2,1,0:T(8,128)(2,1)}) %all-gather.11.cloned.1.call-update) | async-done | bytes 1638416 | tf_op jit(solution)/shard_map/all_gather | solution.py:60
  163.0 3.1 convolution_convert_fusion.11
  167.9 3.3 fusion.140
  173.8 18.1 %all-gather.17.cloned.1.call-done = bf16[2,1280,320]{2,1,0:T(8,128)(2,1)} async-done(((bf16[2,160,320]{2,1,0:T(8,128)(2,1)}), bf16[2,1280,320]{2,1,0:T(8,128)(2,1)}) %all-gather.17.cloned.1.call-update) | async-done | bytes 1638416 | tf_op jit(solution)/shard_map/all_gather | solution.py:61
  192.0 4.3 convolution_convert_fusion.3
  196.6 4.7 copy.97
  201.3 5.1 reshape.145
  206.4 47.9 %all_to_all.129 = bf16[4,2,51200]{2,1,0:T(2,128)(2,1)} all-to-all(bf16[4,2,51200]{2,1,0:T(2,128)(2,1)} %reshape.145), channel_id=1, replica_groups=mesh['rep'=8,'tp'=4] {'tp'}, dimensions={0} | all-to-all | bytes 1638400 | tf_op jit(solution)/shard_map/all_to_all | solution.py:53
  254.2 5.0 reshape.146
  259.3 4.3 copy.117
  265.8 4.7 copy.100
  270.6 5.1 reshape.147
  275.6 47.5 %all_to_all.130 = bf16[4,2,51200]{2,1,0:T(2,128)(2,1)} all-to-all(bf16[4,2,51200]{2,1,0:T(2,128)(2,1)} %reshape.147), channel_id=1, replica_groups=mesh['rep'=8,'tp'=4] {'tp'}, dimensions={0} | all-to-all | bytes 1638400 | tf_op jit(solution)/shard_map/all_to_all | solution.py:54
  323.2 5.0 reshape.148
  328.2 4.3 copy.118
  334.7 4.7 copy.103
  339.4 5.1 reshape.135
  344.5 25.6 %all_to_all.131 = bf16[4,2,51200]{2,1,0:T(2,128)(2,1)} all-to-all(bf16[4,2,51200]{2,1,0:T(2,128)(2,1)} %reshape.135), channel_id=1, replica_groups=mesh['rep'=8,'tp'=4] {'tp'}, dimensions={0} | all-to-all | bytes 1638400 | tf_op jit(solution)/shard_map/all_to_all | solution.py:55
  370.2 5.0 reshape.136
  375.2 4.3 copy.119
  381.8 4.0 fusion.42
  385.8 3.7 multiply_reduce_fusion.2
  389.5 2.8 multiply_convert_fusion.2
  392.4 8.8 fusion.26
  401.2 29.3 %all-gather.21.cloned.1.call-done = bf16[2,1280,1280]{2,1,0:T(8,128)(2,1)} async-done(((bf16[2,160,1280]{2,1,0:T(8,128)(2,1)}), bf16[2,1280,1280]{2,1,0:T(8,128)(2,1)}) %all-gather.21.cloned.1.call-update) | async-done | bytes 6553616 | tf_op jit(solution)/shard_map/all_gather | solution.py:63
  430.5 48.4 %all-gather.23.cloned.1.call-done = bf16[2,1280,1280]{2,1,0:T(8,128)(2,1)} async-done(((bf16[2,160,1280]{2,1,0:T(8,128)(2,1)}), bf16[2,1280,1280]{2,1,0:T(8,128)(2,1)}) %all-gather.23.cloned.1.call-update) | async-done | bytes 6553616 | tf_op jit(solution)/shard_map/all_gather | solution.py:64
  478.9 23.3 %convolution_convert_fusion.2 = bf16[1024,1280]{1,0:T(8,128)(2,1)} fusion(bf16[2,1280,1280]{2,1,0:T(8,128)(2,1)} %all-gather.23.cloned.1.call-done, f32[1024,1280]{1,0:T(8,128)} %fusion.26, bf16[1024,1280]{1,0:T(8,128)(2,1)} %multiply_convert_fusion.2, bf16[2,1280,1280]{2,1,0:T(8,128)(2,1)} %all-gather.21.cloned.1.call-done), kind=kOutput, calls=%fused_computation.57 | convolution fusion | flops 6798704640 | bytes 17039360 | tf_op jit(solution)/shard_map/dot_general | solution.py:89
  502.3 104.2 %all-reduce.7.cloned.1.call-done = bf16[1024,1280]{1,0:T(8,128)(2,1)} async-done(((bf16[1024,1280]{1,0:T(8,128)(2,1)}), bf16[1024,1280]{1,0:T(8,128)(2,1)}) %all-reduce.7.cloned.1.call-update) | async-done | bytes 2621456 | tf_op jit(solution)/shard_map/psum | solution.py:125
  606.5 4.2 fusion.138
  618.1 3.1 convolution_convert_fusion.5
  623.6 3.1 convolution_convert_fusion.7
  628.5 3.3 fusion.145
  634.6 3.1 convolution_convert_fusion.1
  637.8 103.2 %all-reduce.9.cloned.1.call-done = bf16[1024,1280]{1,0:T(8,128)(2,1)} async-done(((bf16[1024,1280]{1,0:T(8,128)(2,1)}), bf16[1024,1280]{1,0:T(8,128)(2,1)}) %all-reduce.9.cloned.1.call-update) | async-done | bytes 2621456 | tf_op jit(solution)/shard_map/psum | solution.py:125
  741.0 3.9 fusion.137
  747.2 7.9 fusion.25
  755.1 24.4 %convolution_convert_fusion = bf16[1024,1280]{1,0:T(8,128)(2,1)} fusion(bf16[2,1280,1280]{2,1,0:T(8,128)(2,1)} %all-gather.23.cloned.1.call-done, f32[1024,1280]{1,0:T(8,128)} %fusion.25, bf16[2,1280,1280]{2,1,0:T(8,128)(2,1)} %all-gather.21.cloned.1.call-done, f32[1024,1280]{1,0:T(8,128)} %copy-done.5, f32[1280]{0:T(1024)S(1)} %get-tuple-element.5, ...), kind=kOutput, calls=%fused_computation.55 | convolution fusion | flops 6803947520 | bytes 19674112 | tf_op jit(solution)/shard_map/dot_general | solution.py:89
  779.4 103.2 %all-reduce.11.cloned.1.call-done = bf16[1024,1280]{1,0:T(8,128)(2,1)} async-done(((bf16[1024,1280]{1,0:T(8,128)(2,1)}), bf16[1024,1280]{1,0:T(8,128)(2,1)}) %all-reduce.11.cloned.1.call-update) | async-done | bytes 2621456 | tf_op jit(solution)/shard_map/psum | solution.py:125
  (122 shorter events, 59.8 us)
Async XLA Ops:
  6.5 85.3 %copy-start = (f32[32,1280]{1,0:T(8,128)S(1)}, f32[32,1280]{1,0:T(8,128)}, u32[]{:S(2)}) copy-start(f32[32,1280]{1,0:T(8,128)} %param.16) | copy-start | bytes 491524
  6.5 19.6 %copy-start.6 = (bf16[2,40,1280]{2,1,0:T(8,128)(2,1)S(1)}, bf16[2,40,1280]{2,1,0:T(8,128)(2,1)}, u32[]{:S(2)}) copy-start(bf16[2,40,1280]{2,1,0:T(8,128)(2,1)} %param.20) | copy-start | bytes 614404
  6.5 43.5 %copy-start.7 = (bf16[2,40,1280]{2,1,0:T(8,128)(2,1)S(1)}, bf16[2,40,1280]{2,1,0:T(8,128)(2,1)}, u32[]{:S(2)}) copy-start(bf16[2,40,1280]{2,1,0:T(8,128)(2,1)} %param.21) | copy-start | bytes 614404
  6.5 85.3 %all-gather.9.cloned.1.call-start = ((), (), s32[]{:S(2)}) async-start(), calls=%async_computation.7 | async-start | bytes 3276800 | tf_op jit(solution)/shard_map/all_gather | solution.py:118
  7.3 97.5 %all-gather.13.cloned.1.call-start = ((), (), s32[]{:S(2)}) async-start(), calls=%async_computation.9 | async-start | bytes 2211840 | tf_op jit(solution)/shard_map/all_gather | solution.py:58
  24.6 44.4 %copy-start.8 = (bf16[2,40,1280]{2,1,0:T(8,128)(2,1)S(1)}, bf16[2,40,1280]{2,1,0:T(8,128)(2,1)}, u32[]{:S(2)}) copy-start(bf16[2,40,1280]{2,1,0:T(8,128)(2,1)} %param.22) | copy-start | bytes 614404
  26.1 107.8 %all-gather.15.cloned.1.call-start = ((), (), s32[]{:S(2)}) async-start(), calls=%async_computation.10 | async-start | bytes 2211840 | tf_op jit(solution)/shard_map/all_gather | solution.py:59
  26.7 48.7 %copy-start.12 = (s32[4]{0:T(128)S(1)}, s32[4]{0:T(128)}, u32[]{:S(2)}) copy-start(s32[4]{0:T(128)} %param.15) | copy-start | bytes 52
  26.7 48.8 %copy-start.11 = (s32[4,4]{1,0:T(4,128)S(1)}, s32[4,4]{1,0:T(4,128)}, u32[]{:S(2)}) copy-start(s32[4,4]{1,0:T(4,128)} %param.14) | copy-start | bytes 196
  26.7 48.9 %copy-start.9 = (f32[2,1280]{1,0:T(2,128)S(1)}, f32[2,1280]{1,0:T(2,128)}, u32[]{:S(2)}) copy-start(f32[2,1280]{1,0:T(2,128)} %param.17) | copy-start | bytes 30724
  50.0 112.9 %all-gather.11.cloned.1.call-start = ((), (), s32[]{:S(2)}) async-start(), calls=%async_computation.8 | async-start | bytes 2211840 | tf_op jit(solution)/shard_map/all_gather | solution.py:60
  71.3 15.0 %all-to-all-start.3 = ((bf16[4,2,12800]{2,1,0:T(2,128)(2,1)}), bf16[4,2,12800]{2,1,0:T(2,128)(2,1)}, u32[]{:S(2)}, u32[]{:S(2)}) async-start(bf16[4,2,12800]{2,1,0:T(2,128)(2,1)} %reshape.143), calls=%async_computation.3 | async-start | bytes 409600 | tf_op jit(solution)/shard_map/all_to_all | solution.py:52
  75.3 116.7 %all-gather.17.cloned.1.call-start = ((), (), s32[]{:S(2)}) async-start(), calls=%async_computation.11 | async-start | bytes 2211840 | tf_op jit(solution)/shard_map/all_gather | solution.py:61
  91.6 290.2 %all-reduce.5.cloned.1.call-start = ((), (), s32[]{:S(2)}) async-start(), calls=%async_computation.12 | async-start | bytes 5242880 | tf_op jit(solution)/shard_map/psum | solution.py:125
  97.0 2.3 copy-start.2
  196.3 196.1 %all-gather.19.cloned.1.call-start = ((), (), s32[]{:S(2)}) async-start(), calls=%async_computation.13 | async-start | bytes 7372800 | tf_op jit(solution)/shard_map/all_gather | solution.py:62
  265.8 164.7 %all-gather.21.cloned.1.call-start = ((), (), s32[]{:S(2)}) async-start(), calls=%async_computation.14 | async-start | bytes 7372800 | tf_op jit(solution)/shard_map/all_gather | solution.py:63
  334.7 144.3 %all-gather.23.cloned.1.call-start = ((), (), s32[]{:S(2)}) async-start(), calls=%async_computation.15 | async-start | bytes 7372800 | tf_op jit(solution)/shard_map/all_gather | solution.py:64
  344.5 37.2 %copy-start.10 = (f32[2,1280]{1,0:T(2,128)S(1)}, f32[2,1280]{1,0:T(2,128)}, u32[]{:S(2)}) copy-start(f32[2,1280]{1,0:T(2,128)} %param.18) | copy-start | bytes 30724
  381.6 224.9 %all-reduce.7.cloned.1.call-start = ((), (), s32[]{:S(2)}) async-start(), calls=%async_computation.16 | async-start | bytes 5242880 | tf_op jit(solution)/shard_map/psum | solution.py:125
  381.8 4.1 copy-start.4
  381.8 7.7 slice-start
  385.8 3.7 slice-start.1
  502.3 238.7 %all-reduce.9.cloned.1.call-start = ((), (), s32[]{:S(2)}) async-start(), calls=%async_computation.17 | async-start | bytes 5242880 | tf_op jit(solution)/shard_map/psum | solution.py:125
  610.7 2.3 copy-start.3
  611.4 2.7 copy-start.13
  631.8 2.7 copy-start.14
  637.8 244.9 %all-reduce.11.cloned.1.call-start = ((), (), s32[]{:S(2)}) async-start(), calls=%async_computation.18 | async-start | bytes 5242880 | tf_op jit(solution)/shard_map/psum | solution.py:125
  744.9 2.3 copy-start.5
  755.0 130.1 %copy-start.1 = (f32[32,1280]{1,0:T(8,128)S(1)}, f32[32,1280]{1,0:T(8,128)}, u32[]{:S(2)}) copy-start(f32[32,1280]{1,0:T(8,128)} %param.16) | copy-start | bytes 491524
Sparse Core Ops, SparseCore 0:
  8.9 66.1 all-gather.8
  77.0 27.7 all-gather.12
  106.7 27.2 all-gather.14
  135.7 27.2 all-gather.10
  164.7 27.2 all-gather.16
  196.4 138.2 all-reduce.4
  336.6 45.3 all-gather.18
  384.0 46.4 all-gather.20
  432.4 46.4 all-gather.22
  502.4 104.0 all-reduce.6
  637.9 103.0 all-reduce.8
  779.6 103.0 all-reduce.10
where the time goes:
time: 902 us; the launch traced here: 892 us
  waiting for transfers between devices  460 us (51%)
  blocking collectives  169 us (19%)
  matrix products  105 us (12%)
  local copies, waits for them, and re-layouts  103 us (11%)
  other arithmetic  35.2 us (4%)
  between operations  14.7 us (2%)
    psum x4, waiting for transfers between devices, total_terms(): lax.psum(partial_value.astype(jnp.bfloat16), 'tp').astype(jnp.float32)  311 us
    unnamed x57, local copies, waits for them, and re-layouts  62.7 us
    dot_general x4, matrix products, out_terms(): lax.dot_general(mixed_rows, weight, (((1,), (1,)), ((), ())), preferred_e...  55.2 us
    all_gather x1, waiting for transfers between devices, reshard(): lax.all_gather(owned[6], 'rep', axis=1, tiled=True)  48.4 us
    all_to_all x1, blocking collectives, reshard(): lax.all_to_all(weights[4], 'tp', split_axis=2, concat_axis=1, tiled=True)  47.9 us
    all_to_all x1, blocking collectives, reshard(): lax.all_to_all(weights[5], 'tp', split_axis=2, concat_axis=1, tiled=True)  47.5 us
    all_gather x1, waiting for transfers between devices, reshard(): lax.all_gather(owned[5], 'rep', axis=1, tiled=True)  29.3 us
    all_to_all x1, blocking collectives, reshard(): lax.all_to_all(weights[6], 'tp', split_axis=2, concat_axis=1, tiled=True)  25.6 us
  transfers between devices with their start and end apart: 13, of which 9 were waited for; matrix products, arithmetic and copies ran while one was open for 16% of the time, Pallas kernels for 0%

commit v1 on v0

v1 whole, which is shorter than its diff:
```python
import math

import jax
import jax.numpy as jnp
from jax import lax
from jax.sharding import PartitionSpec as P

HEADS = 8
VIEWS = 4
HW = 64
PAIR = 2


def layer_norm(activations, gain_vector):
    average = jnp.mean(activations, axis=-1, keepdims=True)
    centred = activations - average
    spread = jnp.mean(centred * centred, axis=-1, keepdims=True)
    return (centred * lax.rsqrt(spread + 1e-05) * gain_vector).astype(jnp.bfloat16)


def time_code(step_ids, width):
    half_width = width // 2
    frequency = jnp.exp(-math.log(10000.0) * jnp.arange(half_width, dtype=jnp.float32) / half_width)
    angles = step_ids.astype(jnp.float32)[:, None] * frequency[None, :]
    return jnp.concatenate([jnp.cos(angles), jnp.sin(angles)], axis=1)


def conditioning(share_rows, view_ids, time_ids, camera_table):
    slot_count = share_rows // HW
    slot_ids = lax.axis_index("tp") * slot_count + jnp.arange(slot_count, dtype=jnp.int32)
    flat_views = view_ids.reshape(-1)
    slot_range = jnp.arange(flat_views.shape[0], dtype=jnp.int32)
    pose_ids = jnp.sum(
        jnp.where(slot_ids[:, None] == slot_range[None, :], flat_views[None, :], 0), axis=1
    )
    set_range = jnp.arange(time_ids.shape[0], dtype=jnp.int32)
    step_ids = jnp.sum(
        jnp.where((slot_ids // VIEWS)[:, None] == set_range[None, :], time_ids[None, :], 0), axis=1
    )
    pose_range = jnp.arange(camera_table.shape[0], dtype=jnp.int32)
    onehot_pose = (pose_ids[:, None] == pose_range[None, :]).astype(jnp.float32)
    camera = jnp.dot(onehot_pose, camera_table, precision=lax.Precision.HIGHEST)
    return camera + time_code(step_ids, camera_table.shape[1])


def exchange(value, step, count):
    return lax.ppermute(value, "tp", [(i, i ^ step) for i in range(count)])


def column_halves(shards):
    def pack(part):
        pieces = []
        for shard in shards:
            half = shard.shape[1] // PAIR
            pieces.append(shard[:, part * half : (part + 1) * half])
        return jnp.concatenate(pieces, axis=1)

    return pack(0), pack(1)


def gather_pack(shards, tp_index, tp_count):
    first, second = column_halves(shards)
    lower = tp_index % PAIR == 0
    mine = jnp.where(lower, first, second)
    other = jnp.where(lower, second, first)
    rows, columns = mine.shape
    stacked = jnp.zeros((tp_count, rows, columns), mine.dtype)
    stacked = lax.dynamic_update_slice(stacked, mine[None], (tp_index, 0, 0))
    for step in range(1, tp_count):
        arrived = exchange(mine if step % PAIR == 0 else other, step, tp_count)
        stacked = lax.dynamic_update_slice(stacked, arrived[None], (tp_index ^ step, 0, 0))
    return lax.all_gather(stacked.reshape(tp_count * rows, columns), "rep", axis=0, tiled=True)


def attend(packed, head_count, head_size):
    total_rows = packed.shape[0]
    seq_len = VIEWS * HW
    width = head_count * head_size
    shape_heads = (total_rows // seq_len, seq_len, head_count, head_size)
    query_rows = packed[:, :width].reshape(shape_heads)
    key_rows = packed[:, width : 2 * width].reshape(shape_heads)
    value_rows = packed[:, 2 * width :].reshape(shape_heads)
    scores = jnp.einsum(
        "bqhd,bkhd->bhqk", query_rows, key_rows, preferred_element_type=jnp.float32
    ) * head_size ** (-0.5)
    peak = jnp.max(scores, axis=-1, keepdims=True)
    expons = jnp.exp(scores - peak)
    attn_probs = (expons / jnp.sum(expons, axis=-1, keepdims=True)).astype(jnp.bfloat16)
    mixed_rows = jnp.einsum(
        "bhqk,bkhd->bqhd", attn_probs, value_rows, preferred_element_type=jnp.float32
    )
    return mixed_rows.astype(jnp.bfloat16).reshape(total_rows, width)


def transposed_dot(left, right):
    return lax.dot_general(
        left, right, (((1,), (1,)), ((), ())), preferred_element_type=jnp.float32
    )


def body(
    tokens,
    view_ids,
    time_ids,
    camera_table,
    norm_attn,
    norm_ffn,
    w_query,
    w_key,
    w_value,
    w_out,
    w_gate,
    w_up,
    w_down,
):
    tp_count = lax.axis_size("tp")
    tp_index = lax.axis_index("tp")
    share_rows, channels = tokens.shape
    layers = w_query.shape[0]
    head_count = HEADS // PAIR
    head_size = channels // HEADS
    width = head_count * head_size
    inner = w_gate.shape[2] // PAIR

    attn_packs = []
    ffn_packs = []
    for layer in range(layers):
        attn_packs.append(
            gather_pack(
                [w_query[layer], w_key[layer], w_value[layer], w_out[layer]], tp_index, tp_count
            )
        )
        ffn_packs.append(
            gather_pack([w_gate[layer], w_up[layer], w_down[layer]], tp_index, tp_count)
        )

    slots = conditioning(share_rows, view_ids, time_ids, camera_table)
    stream = (
        tokens.astype(jnp.float32).reshape(-1, HW, channels) + slots[:, None, :]
    ).reshape(share_rows, channels)

    def pair_update(stream, partial_rows):
        arrived = exchange(partial_rows[share_rows:].astype(jnp.bfloat16), 1, tp_count)
        return stream + partial_rows[:share_rows] + arrived.astype(jnp.float32)

    for layer in range(layers):
        attn_w = attn_packs[layer]
        ffn_w = ffn_packs[layer]
        normed = layer_norm(stream, norm_attn[layer])
        rows = jnp.concatenate([normed, exchange(normed, 1, tp_count)], axis=0)
        packed = jnp.dot(
            rows, attn_w[:, : 3 * width], preferred_element_type=jnp.float32
        ).astype(jnp.bfloat16)
        mixed = attend(packed, head_count, head_size)
        stream = pair_update(stream, transposed_dot(mixed, attn_w[:, 3 * width :]))
        normed = layer_norm(stream, norm_ffn[layer])
        rows = jnp.concatenate([normed, exchange(normed, 1, tp_count)], axis=0)
        gate_part = jnp.dot(rows, ffn_w[:, :inner], preferred_element_type=jnp.float32)
        up_part = jnp.dot(rows, ffn_w[:, inner : 2 * inner], preferred_element_type=jnp.float32)
        hidden = (jax.nn.gelu(gate_part, approximate=False) * up_part).astype(jnp.bfloat16)
        hidden = lax.optimization_barrier(hidden)
        stream = pair_update(stream, transposed_dot(hidden, ffn_w[:, 2 * inner :]))
    return stream.astype(jnp.bfloat16)


def solution(mesh):
    return jax.shard_map(
        body,
        mesh=mesh,
        in_specs=(
            P(("rep", "tp"), None),
            P("rep", None),
            P("rep"),
            P(),
            P(),
            P(),
            P(None, ("rep", "tp"), None),
            P(None, ("rep", "tp"), None),
            P(None, ("rep", "tp"), None),
            P(None, ("rep", "tp"), None),
            P(None, ("rep", "tp"), None),
            P(None, ("rep", "tp"), None),
            P(None, ("rep", "tp"), None),
        ),
        out_specs=P(("rep", "tp"), None),
        check_vma=False,
    )
```

time: 902 us -> 412 us (0.46)
  waiting for transfers between devices: 460 us -> 246 us
  blocking collectives: 169 us -> 0 us
  local copies, waits for them, and re-layouts: 103 us -> 41.5 us
  matrix products: 105 us -> 75.9 us
  other arithmetic: 35.2 us -> 7.95 us
  starting transfers between devices: 4.85 us -> 20 us
    psum x4 -> x0, waiting for transfers between devices: 311 us -> none  [total_terms(): lax.psum(partial_value.astype(jnp.bfloat16), 'tp').astype(jnp.float32)]
    ppermute x0 -> x20, waiting for transfers between devices: none -> 229 us  [exchange(): return lax.ppermute(value, 'tp', [(i, i ^ step) for i in range(count)])]
    all_to_all x6 -> x0, blocking collectives: 169 us -> none  [the longest x1 47.9 us: reshard(): lax.all_to_all(weights[4], 'tp', split_axis=2, concat_axis=1, tiled=True)]
    all_gather x8 -> x4, waiting for transfers between devices: 148 us -> 16.7 us  [gather_pack(): lax.all_gather(stacked.reshape(tp_count * rows, columns), 'rep', axis=0,...]
    unnamed x57 -> x80, local copies, waits for them, and re-layouts: 62.7 us -> 11 us
    all_to_all x14 -> x0, local copies, waits for them, and re-layouts: 27 us -> none  [the longest x2 6.48 us: reshard(): lax.all_to_all(weights[4], 'tp', split_axis=2, concat_axis=1, tiled=True)]
    dot_general x12, matrix products: 89.2 us -> 68.1 us  [the longest x2 28.1 us: body(): jnp.dot(rows, ffn_w[:, inner:2 * inner], preferred_element_type=jnp.float32)]
    ppermute x0 -> x20, starting transfers between devices: none -> 19.9 us  [exchange(): return lax.ppermute(value, 'tp', [(i, i ^ step) for i in range(count)])]
  transfers between devices with their start and end apart: 13 -> 24, of which waited for: 9 -> 16; matrix products, arithmetic and copies ran while one was open for 16% -> 20% of each run, Pallas kernels for 0% -> 0%
where the time goes in v1:
time: 412 us; the launch traced here: 406 us
  waiting for transfers between devices  246 us (60%)
  matrix products  75.9 us (18%)
  local copies, waits for them, and re-layouts  41.5 us (10%)
  starting transfers between devices  20 us (5%)
  between operations  14.6 us (4%)
  other arithmetic  7.95 us (2%)
    ppermute x20, waiting for transfers between devices, exchange(): return lax.ppermute(value, 'tp', [(i, i ^ step) for i in range(count)])  229 us
    dot_general x2, matrix products, body(): jnp.dot(rows, ffn_w[:, inner:2 * inner], preferred_element_type=jnp.float32)  28.1 us
    ppermute x20, starting transfers between devices, exchange(): return lax.ppermute(value, 'tp', [(i, i ^ step) for i in range(count)])  19.9 us
    all_gather x4, waiting for transfers between devices, gather_pack(): lax.all_gather(stacked.reshape(tp_count * rows, columns), 'rep', axis=0,...  16.7 us
    dot_general x4, matrix products, transposed_dot(): lax.dot_general(left, right, (((1,), (1,)), ((), ())), preferred_element_...  12.5 us
    dot_general x2, matrix products, body(): jnp.dot(rows, attn_w[:, :3 * width], preferred_element_type=jnp.float32)  12 us
    dot_general x2, matrix products, body(): jnp.dot(rows, ffn_w[:, :inner], preferred_element_type=jnp.float32)  11.8 us
    unnamed x80, local copies, waits for them, and re-layouts  11 us
  transfers between devices with their start and end apart: 24, of which 16 were waited for; matrix products, arithmetic and copies ran while one was open for 20% of the time, Pallas kernels for 0%

profile of v1, /device:TPU:0, one launch (start us, length us, event | category | flops | bytes accessed | tf_op | source)
XLA Modules:
  0.0 406.2 jit_solution(8337535634784881402)
XLA Ops:
  14.1 3.1 collective-permute-start.1
  17.1 2.5 collective-permute-start.3
  19.9 3.0 collective-permute-done.1
  22.9 15.1 %collective-permute-done.2 = bf16[40,2560]{1,0:T(8,128)(2,1)} collective-permute-done((bf16[40,2560]{1,0:T(8,128)(2,1)}, bf16[40,2560]{1,0:T(8,128)(2,1)}, u32[]{:S(2)}, u32[]{:S(2)}) %collective-permute-start.2) | collective-permute-done | bytes 204832 | tf_op jit(solution)/shard_map/ppermute | solution.py:47
  43.6 2.7 collective-permute-start.8
  47.5 23.2 %collective-permute-done.6 = bf16[40,7680]{1,0:T(8,128)(2,1)S(1)} collective-permute-done((bf16[40,7680]{1,0:T(8,128)(2,1)S(1)}, bf16[40,7680]{1,0:T(8,128)(2,1)S(1)}, u32[]{:S(2)}, u32[]{:S(2)}) %collective-permute-start.6) | collective-permute-done | bytes 614432 | tf_op jit(solution)/shard_map/ppermute | solution.py:47
  70.7 28.3 %collective-permute-done.7 = bf16[40,7680]{1,0:T(8,128)(2,1)S(1)} collective-permute-done((bf16[40,7680]{1,0:T(8,128)(2,1)S(1)}, bf16[40,7680]{1,0:T(8,128)(2,1)S(1)}, u32[]{:S(2)}, u32[]{:S(2)}) %collective-permute-start.7) | collective-permute-done | bytes 614432 | tf_op jit(solution)/shard_map/ppermute | solution.py:47
  99.2 1.5 copy-done.4
  100.9 1.1 broadcast_select_fusion.4
  102.1 2.4 collective-permute-start.13
  105.8 4.2 %collective-permute-done.11 = bf16[40,2560]{1,0:T(8,128)(2,1)S(1)} collective-permute-done((bf16[40,2560]{1,0:T(8,128)(2,1)S(1)}, bf16[40,2560]{1,0:T(8,128)(2,1)S(1)}, u32[]{:S(2)}, u32[]{:S(2)}) %collective-permute-start.11) | collective-permute-done | bytes 204832 | tf_op jit(solution)/shard_map/ppermute | solution.py:47
  110.0 11.3 %collective-permute-done.12 = bf16[40,2560]{1,0:T(8,128)(2,1)S(1)} collective-permute-done((bf16[40,2560]{1,0:T(8,128)(2,1)S(1)}, bf16[40,2560]{1,0:T(8,128)(2,1)S(1)}, u32[]{:S(2)}, u32[]{:S(2)}) %collective-permute-start.12) | collective-permute-done | bytes 204832 | tf_op jit(solution)/shard_map/ppermute | solution.py:47
  122.7 2.1 collective-permute-start.18
  124.8 1.4 collective-permute-start.17
  126.6 22.5 %collective-permute-done.16 = bf16[40,7680]{1,0:T(8,128)(2,1)S(1)} collective-permute-done((bf16[40,7680]{1,0:T(8,128)(2,1)S(1)}, bf16[40,7680]{1,0:T(8,128)(2,1)S(1)}, u32[]{:S(2)}, u32[]{:S(2)}) %collective-permute-start.16) | collective-permute-done | bytes 614432 | tf_op jit(solution)/shard_map/ppermute | solution.py:47
  149.2 28.2 %collective-permute-done.17 = bf16[40,7680]{1,0:T(8,128)(2,1)S(1)} collective-permute-done((bf16[40,7680]{1,0:T(8,128)(2,1)S(1)}, bf16[40,7680]{1,0:T(8,128)(2,1)S(1)}, u32[]{:S(2)}, u32[]{:S(2)}) %collective-permute-start.17) | collective-permute-done | bytes 614432 | tf_op jit(solution)/shard_map/ppermute | solution.py:47
  177.5 1.4 copy-done.3
  180.8 13.7 %collective-permute-done = bf16[256,1280]{1,0:T(8,128)(2,1)S(1)} collective-permute-done((bf16[256,1280]{1,0:T(8,128)(2,1)S(1)}, bf16[256,1280]{1,0:T(8,128)(2,1)S(1)}, u32[]{:S(2)}, u32[]{:S(2)}) %collective-permute-start) | collective-permute-done | bytes 655392 | tf_op jit(solution)/shard_map/ppermute | solution.py:47
  194.5 5.3 %fusion.40 = bf16[512,1920]{1,0:T(8,128)(2,1)S(1)} fusion(bf16[1280,2560]{1,0:T(8,128)(2,1)} %all-gather.5.cloned.1.call-done, bf16[256,1280]{1,0:T(8,128)(2,1)S(1)} %collective-permute-done, bf16[256,1280]{1,0:T(8,128)(2,1)S(1)} %multiply_convert_fusion.3), kind=kOutput, calls=%fused_computation.58 | convolution fusion | flops 2520186880 | bytes 8192000 | tf_op jit(solution)/shard_map/dot_general | solution.py:151
  199.8 1.2 fusion.131
  201.8 3.3 reshape.514
  205.1 3.6 reshape.512
  209.5 1.8 fusion.71
  211.4 3.1 fusion.65
  215.3 2.7 fusion.50
  218.5 13.6 %collective-permute-done.4 = bf16[256,1280]{1,0:T(8,128)(2,1)S(1)} collective-permute-done((bf16[256,1280]{1,0:T(8,128)(2,1)S(1)}, bf16[256,1280]{1,0:T(8,128)(2,1)S(1)}, u32[]{:S(2)}, u32[]{:S(2)}) %collective-permute-start.4) | collective-permute-done | bytes 655392 | tf_op jit(solution)/shard_map/ppermute | solution.py:47
  233.3 11.7 %collective-permute-done.5 = bf16[256,1280]{1,0:T(8,128)(2,1)S(1)} collective-permute-done((bf16[256,1280]{1,0:T(8,128)(2,1)S(1)}, bf16[256,1280]{1,0:T(8,128)(2,1)S(1)}, u32[]{:S(2)}, u32[]{:S(2)}) %collective-permute-start.5) | collective-permute-done | bytes 655392 | tf_op jit(solution)/shard_map/ppermute | solution.py:47
  245.0 5.9 %fusion.12 = f32[512,2560]{1,0:T(8,128)S(1)} fusion(bf16[1280,7680]{1,0:T(8,128)(2,1)} %all-gather.7.cloned.1.call-done, bf16[256,1280]{1,0:T(8,128)(2,1)S(1)} %collective-permute-done.5, bf16[256,1280]{1,0:T(8,128)(2,1)S(1)} %multiply_convert_fusion.2), kind=kOutput, calls=%fused_computation.14 | convolution fusion | flops 3358064640 | bytes 13107200 | tf_op jit(solution)/shard_map/dot_general | solution.py:158
  251.0 2.8 copy-done.36
  253.8 14.0 %fusion.17 = bf16[512,2560]{1,0:T(8,128)(2,1)S(1)} fusion(f32[512,2560]{1,0:T(8,128)S(1)} %fusion.12, bf16[1280,7680]{1,0:T(8,128)(2,1)S(1)} %copy-done.36, bf16[256,1280]{1,0:T(8,128)(2,1)S(1)} %collective-permute-done.5, bf16[256,1280]{1,0:T(8,128)(2,1)S(1)} %multiply_convert_fusion.2), kind=kOutput, calls=%fused_computation.19 | convolution fusion | flops 3444572160 | bytes 15728640 | tf_op jit(solution)/shard_map/dot_general | solution.py:159
  267.8 3.6 fusion.8
  272.0 13.4 %collective-permute-done.9 = bf16[256,1280]{1,0:T(8,128)(2,1)S(1)} collective-permute-done((bf16[256,1280]{1,0:T(8,128)(2,1)S(1)}, bf16[256,1280]{1,0:T(8,128)(2,1)S(1)}, u32[]{:S(2)}, u32[]{:S(2)}) %collective-permute-start.9) | collective-permute-done | bytes 655392 | tf_op jit(solution)/shard_map/ppermute | solution.py:47
  286.8 10.1 %collective-permute-done.10 = bf16[256,1280]{1,0:T(8,128)(2,1)S(1)} collective-permute-done((bf16[256,1280]{1,0:T(8,128)(2,1)S(1)}, bf16[256,1280]{1,0:T(8,128)(2,1)S(1)}, u32[]{:S(2)}, u32[]{:S(2)}) %collective-permute-start.10) | collective-permute-done | bytes 655392 | tf_op jit(solution)/shard_map/ppermute | solution.py:47
  296.9 6.7 %fusion.43 = bf16[512,1920]{1,0:T(8,128)(2,1)S(1)} fusion(bf16[1280,2560]{1,0:T(8,128)(2,1)} %all-gather.9.cloned.1.call-done, bf16[256,1280]{1,0:T(8,128)(2,1)S(1)} %collective-permute-done.10, bf16[256,1280]{1,0:T(8,128)(2,1)S(1)} %multiply_convert_fusion.1), kind=kOutput, calls=%fused_computation.59 | convolution fusion | flops 2520186880 | bytes 8192000 | tf_op jit(solution)/shard_map/dot_general | solution.py:151
  303.6 1.2 fusion.130
  305.6 3.0 reshape.517
  308.6 3.6 reshape.515
  313.0 1.8 fusion.67
  314.8 2.8 fusion.66
  318.5 2.7 fusion.48
  321.3 15.9 %collective-permute-done.14 = bf16[256,1280]{1,0:T(8,128)(2,1)S(1)} collective-permute-done((bf16[256,1280]{1,0:T(8,128)(2,1)S(1)}, bf16[256,1280]{1,0:T(8,128)(2,1)S(1)}, u32[]{:S(2)}, u32[]{:S(2)}) %collective-permute-start.14) | collective-permute-done | bytes 655392 | tf_op jit(solution)/shard_map/ppermute | solution.py:47
  338.2 16.7 %all-gather.11.cloned.1.call-done = bf16[1280,7680]{1,0:T(8,128)(2,1)} async-done(((bf16[160,7680]{1,0:T(8,128)(2,1)}), bf16[1280,7680]{1,0:T(8,128)(2,1)}) %all-gather.11.cloned.1.call-update) | async-done | bytes 19660816 | tf_op jit(solution)/shard_map/all_gather | solution.py:72
  354.9 5.8 %fusion.6 = f32[512,2560]{1,0:T(8,128)S(1)} fusion(bf16[1280,7680]{1,0:T(8,128)(2,1)} %all-gather.11.cloned.1.call-done, bf16[256,1280]{1,0:T(8,128)(2,1)S(1)} %collective-permute-done.15, bf16[256,1280]{1,0:T(8,128)(2,1)S(1)} %multiply_convert_fusion), kind=kOutput, calls=%fused_computation.8 | convolution fusion | flops 3358064640 | bytes 13107200 | tf_op jit(solution)/shard_map/dot_general | solution.py:158
  360.8 2.7 copy-done.37
  363.4 14.1 %fusion.21 = bf16[512,2560]{1,0:T(8,128)(2,1)S(1)} fusion(f32[512,2560]{1,0:T(8,128)S(1)} %fusion.6, bf16[1280,7680]{1,0:T(8,128)(2,1)S(1)} %copy-done.37, bf16[256,1280]{1,0:T(8,128)(2,1)S(1)} %collective-permute-done.15, bf16[256,1280]{1,0:T(8,128)(2,1)S(1)} %multiply_convert_fusion), kind=kOutput, calls=%fused_computation.23 | convolution fusion | flops 3444572160 | bytes 15728640 | tf_op jit(solution)/shard_map/dot_general | solution.py:159
  377.5 3.6 fusion.2
  381.2 1.6 collective-permute-start.19
  382.7 15.4 %collective-permute-done.19 = bf16[256,1280]{1,0:T(8,128)(2,1)S(1)} collective-permute-done((bf16[256,1280]{1,0:T(8,128)(2,1)S(1)}, bf16[256,1280]{1,0:T(8,128)(2,1)S(1)}, u32[]{:S(2)}, u32[]{:S(2)}) %collective-permute-start.19) | collective-permute-done | bytes 655392 | tf_op jit(solution)/shard_map/ppermute | solution.py:47
  (183 shorter events, 30.4 us)
Async XLA Ops:
  6.5 173.1 %copy-start = (f32[32,1280]{1,0:T(8,128)S(1)}, f32[32,1280]{1,0:T(8,128)}, u32[]{:S(2)}) copy-start(f32[32,1280]{1,0:T(8,128)} %param.16) | copy-start | bytes 491524
  6.5 13.2 %copy-start.12 = (bf16[2,40,5120]{2,1,0:T(8,128)(2,1)S(1)}, bf16[2,40,5120]{2,1,0:T(8,128)(2,1)}, u32[]{:S(2)}) copy-start(bf16[2,40,5120]{2,1,0:T(8,128)(2,1)} %param.23) | copy-start | bytes 2457604
  6.5 188.0 %all-gather.5.cloned.1.call-start = ((), (), s32[]{:S(2)}) async-start(), calls=%async_computation | async-start | bytes 7372800 | tf_op jit(solution)/shard_map/all_gather | solution.py:72
  14.1 8.8 %collective-permute-start.1 = (bf16[40,2560]{1,0:T(8,128)(2,1)}, bf16[40,2560]{1,0:T(8,128)(2,1)S(1)}, u32[]{:S(2)}, u32[]{:S(2)}) collective-permute-start(bf16[40,2560]{1,0:T(8,128)(2,1)} %get-tuple-element.44), channel_id=1, source_target_pairs={{0,1},{1,0},{2,3},{3,2},{4,5},{5,4},{6,7},{7,6},{8,9},{9,8},{10,11... | collective-permute-start | bytes 614408 | tf_op jit(solution)/shard_map/ppermute | solution.py:47
  17.1 21.8 %collective-permute-start.3 = (bf16[40,2560]{1,0:T(8,128)(2,1)}, bf16[40,2560]{1,0:T(8,128)(2,1)S(1)}, u32[]{:S(2)}, u32[]{:S(2)}) collective-permute-start(bf16[40,2560]{1,0:T(8,128)(2,1)} %get-tuple-element.44), channel_id=1, source_target_pairs={{0,3},{1,2},{2,1},{3,0},{4,7},{5,6},{6,5},{7,4},{8,11},{9,10},{10,... | collective-permute-start | bytes 614408 | tf_op jit(solution)/shard_map/ppermute | solution.py:47
  19.6 18.4 %collective-permute-start.2 = (bf16[40,2560]{1,0:T(8,128)(2,1)}, bf16[40,2560]{1,0:T(8,128)(2,1)}, u32[]{:S(2)}, u32[]{:S(2)}) collective-permute-start(bf16[40,2560]{1,0:T(8,128)(2,1)} %get-tuple-element.43), channel_id=1, source_target_pairs={{0,2},{1,3},{2,0},{3,1},{4,6},{5,7},{6,4},{7,5},{8,10},{9,11},{10,... | collective-permute-start | bytes 614408 | tf_op jit(solution)/shard_map/ppermute | solution.py:47
  19.8 21.0 %copy-start.13 = (bf16[2,40,5120]{2,1,0:T(8,128)(2,1)S(1)}, bf16[2,40,5120]{2,1,0:T(8,128)(2,1)}, u32[]{:S(2)}) copy-start(bf16[2,40,5120]{2,1,0:T(8,128)(2,1)} %param.24) | copy-start | bytes 2457604
  39.9 205.1 %all-gather.7.cloned.1.call-start = ((), (), s32[]{:S(2)}) async-start(), calls=%async_computation.1 | async-start | bytes 22118400 | tf_op jit(solution)/shard_map/all_gather | solution.py:72
  43.5 27.1 %collective-permute-start.6 = (bf16[40,7680]{1,0:T(8,128)(2,1)S(1)}, bf16[40,7680]{1,0:T(8,128)(2,1)S(1)}, u32[]{:S(2)}, u32[]{:S(2)}) collective-permute-start(bf16[40,7680]{1,0:T(8,128)(2,1)S(1)} %get-tuple-element.24), channel_id=1, source_target_pairs={{0,1},{1,0},{2,3},{3,2},{4,5},{5,4},{6,7},{7,6},{8,9},{9,8},{10,11... | collective-permute-start | bytes 1843208 | tf_op jit(solution)/shard_map/ppermute | solution.py:47
  43.6 55.5 %collective-permute-start.8 = (bf16[40,7680]{1,0:T(8,128)(2,1)S(1)}, bf16[40,7680]{1,0:T(8,128)(2,1)S(1)}, u32[]{:S(2)}, u32[]{:S(2)}) collective-permute-start(bf16[40,7680]{1,0:T(8,128)(2,1)S(1)} %get-tuple-element.24), channel_id=1, source_target_pairs={{0,3},{1,2},{2,1},{3,0},{4,7},{5,6},{6,5},{7,4},{8,11},{9,10},{10,... | collective-permute-start | bytes 1843208 | tf_op jit(solution)/shard_map/ppermute | solution.py:47
  46.3 52.7 %collective-permute-start.7 = (bf16[40,7680]{1,0:T(8,128)(2,1)S(1)}, bf16[40,7680]{1,0:T(8,128)(2,1)S(1)}, u32[]{:S(2)}, u32[]{:S(2)}) collective-permute-start(bf16[40,7680]{1,0:T(8,128)(2,1)S(1)} %get-tuple-element.23), channel_id=1, source_target_pairs={{0,2},{1,3},{2,0},{3,1},{4,6},{5,7},{6,4},{7,5},{8,10},{9,11},{10,... | collective-permute-start | bytes 1843208 | tf_op jit(solution)/shard_map/ppermute | solution.py:47
  70.7 30.2 %copy-start.26 = (bf16[40,640]{1,0:T(8,128)(2,1)S(1)}, bf16[40,640]{1,0:T(8,128)(2,1)}, u32[]{:S(2)}) copy-start(bf16[40,640]{1,0:T(8,128)(2,1)} %get-tuple-element.101) | copy-start | bytes 153604
  70.7 30.2 %copy-start.27 = (bf16[40,640]{1,0:T(8,128)(2,1)S(1)}, bf16[40,640]{1,0:T(8,128)(2,1)}, u32[]{:S(2)}) copy-start(bf16[40,640]{1,0:T(8,128)(2,1)} %get-tuple-element.104) | copy-start | bytes 153604
  70.7 30.2 %copy-start.30 = (bf16[40,640]{1,0:T(8,128)(2,1)S(1)}, bf16[40,640]{1,0:T(8,128)(2,1)}, u32[]{:S(2)}) copy-start(bf16[40,640]{1,0:T(8,128)(2,1)} %get-tuple-element.105) | copy-start | bytes 153604
  70.7 30.2 %copy-start.31 = (bf16[40,640]{1,0:T(8,128)(2,1)S(1)}, bf16[40,640]{1,0:T(8,128)(2,1)}, u32[]{:S(2)}) copy-start(bf16[40,640]{1,0:T(8,128)(2,1)} %get-tuple-element.108) | copy-start | bytes 153604
  70.7 30.2 %copy-start.32 = (bf16[40,640]{1,0:T(8,128)(2,1)S(1)}, bf16[40,640]{1,0:T(8,128)(2,1)}, u32[]{:S(2)}) copy-start(bf16[40,640]{1,0:T(8,128)(2,1)} %get-tuple-element.109) | copy-start | bytes 153604
  99.1 6.6 %copy-start.21 = (bf16[1,40,640]{2,1,0:T(8,128)(2,1)S(1)}, bf16[1,40,640]{2,1,0:T(8,128)(2,1)}, u32[]{:S(2)}) copy-start(bf16[1,40,640]{2,1,0:T(8,128)(2,1)} %get-tuple-element.103) | copy-start | bytes 153604
  99.1 6.6 %copy-start.22 = (bf16[1,40,640]{2,1,0:T(8,128)(2,1)S(1)}, bf16[1,40,640]{2,1,0:T(8,128)(2,1)}, u32[]{:S(2)}) copy-start(bf16[1,40,640]{2,1,0:T(8,128)(2,1)} %get-tuple-element.106) | copy-start | bytes 153604
  99.1 6.6 %copy-start.23 = (bf16[1,40,640]{2,1,0:T(8,128)(2,1)S(1)}, bf16[1,40,640]{2,1,0:T(8,128)(2,1)}, u32[]{:S(2)}) copy-start(bf16[1,40,640]{2,1,0:T(8,128)(2,1)} %get-tuple-element.107) | copy-start | bytes 153604
  99.1 6.6 %copy-start.24 = (bf16[1,40,640]{2,1,0:T(8,128)(2,1)S(1)}, bf16[1,40,640]{2,1,0:T(8,128)(2,1)}, u32[]{:S(2)}) copy-start(bf16[1,40,640]{2,1,0:T(8,128)(2,1)} %get-tuple-element.110) | copy-start | bytes 153604
  100.7 21.6 %copy-start.15 = (bf16[40,2560]{1,0:T(8,128)(2,1)S(1)}, bf16[40,2560]{1,0:T(8,128)(2,1)}, u32[]{:S(2)}) copy-start(bf16[40,2560]{1,0:T(8,128)(2,1)} %get-tuple-element.31) | copy-start | bytes 614404
  100.7 21.6 %copy-start.16 = (bf16[40,2560]{1,0:T(8,128)(2,1)S(1)}, bf16[40,2560]{1,0:T(8,128)(2,1)}, u32[]{:S(2)}) copy-start(bf16[40,2560]{1,0:T(8,128)(2,1)} %get-tuple-element.34) | copy-start | bytes 614404
  100.8 21.6 %copy-start.17 = (bf16[40,2560]{1,0:T(8,128)(2,1)S(1)}, bf16[40,2560]{1,0:T(8,128)(2,1)}, u32[]{:S(2)}) copy-start(bf16[40,2560]{1,0:T(8,128)(2,1)} %get-tuple-element.35) | copy-start | bytes 614404
  100.8 21.6 %copy-start.18 = (bf16[40,2560]{1,0:T(8,128)(2,1)S(1)}, bf16[40,2560]{1,0:T(8,128)(2,1)}, u32[]{:S(2)}) copy-start(bf16[40,2560]{1,0:T(8,128)(2,1)} %get-tuple-element.38) | copy-start | bytes 614404
  100.8 21.6 %copy-start.19 = (bf16[40,2560]{1,0:T(8,128)(2,1)S(1)}, bf16[40,2560]{1,0:T(8,128)(2,1)}, u32[]{:S(2)}) copy-start(bf16[40,2560]{1,0:T(8,128)(2,1)} %get-tuple-element.39) | copy-start | bytes 614404
  100.8 21.6 %copy-start.20 = (bf16[40,2560]{1,0:T(8,128)(2,1)S(1)}, bf16[40,2560]{1,0:T(8,128)(2,1)}, u32[]{:S(2)}) copy-start(bf16[40,2560]{1,0:T(8,128)(2,1)} %get-tuple-element.42) | copy-start | bytes 614404
  100.8 186.0 %all-gather.9.cloned.1.call-start = ((), (), s32[]{:S(2)}) async-start(), calls=%async_computation.2 | async-start | bytes 7372800 | tf_op jit(solution)/shard_map/all_gather | solution.py:72
  102.0 7.9 %collective-permute-start.11 = (bf16[40,2560]{1,0:T(8,128)(2,1)S(1)}, bf16[40,2560]{1,0:T(8,128)(2,1)S(1)}, u32[]{:S(2)}, u32[]{:S(2)}) collective-permute-start(bf16[40,2560]{1,0:T(8,128)(2,1)S(1)} %get-tuple-element.58), channel_id=1, source_target_pairs={{0,1},{1,0},{2,3},{3,2},{4,5},{5,4},{6,7},{7,6},{8,9},{9,8},{10,11... | collective-permute-start | bytes 614408 | tf_op jit(solution)/shard_map/ppermute | solution.py:47
  102.1 19.2 %collective-permute-start.13 = (bf16[40,2560]{1,0:T(8,128)(2,1)S(1)}, bf16[40,2560]{1,0:T(8,128)(2,1)S(1)}, u32[]{:S(2)}, u32[]{:S(2)}) collective-permute-start(bf16[40,2560]{1,0:T(8,128)(2,1)S(1)} %get-tuple-element.58), channel_id=1, source_target_pairs={{0,3},{1,2},{2,1},{3,0},{4,7},{5,6},{6,5},{7,4},{8,11},{9,10},{10,... | collective-permute-start | bytes 614408 | tf_op jit(solution)/shard_map/ppermute | solution.py:47
  104.5 16.8 %collective-permute-start.12 = (bf16[40,2560]{1,0:T(8,128)(2,1)S(1)}, bf16[40,2560]{1,0:T(8,128)(2,1)S(1)}, u32[]{:S(2)}, u32[]{:S(2)}) collective-permute-start(bf16[40,2560]{1,0:T(8,128)(2,1)S(1)} %get-tuple-element.57), channel_id=1, source_target_pairs={{0,2},{1,3},{2,0},{3,1},{4,6},{5,7},{6,4},{7,5},{8,10},{9,11},{10,... | collective-permute-start | bytes 614408 | tf_op jit(solution)/shard_map/ppermute | solution.py:47
  122.3 232.6 %all-gather.11.cloned.1.call-start = ((), (), s32[]{:S(2)}) async-start(), calls=%async_computation.3 | async-start | bytes 22118400 | tf_op jit(solution)/shard_map/all_gather | solution.py:72
  122.7 26.4 %collective-permute-start.16 = (bf16[40,7680]{1,0:T(8,128)(2,1)S(1)}, bf16[40,7680]{1,0:T(8,128)(2,1)S(1)}, u32[]{:S(2)}, u32[]{:S(2)}) collective-permute-start(bf16[40,7680]{1,0:T(8,128)(2,1)S(1)} %get-tuple-element.22), channel_id=1, source_target_pairs={{0,1},{1,0},{2,3},{3,2},{4,5},{5,4},{6,7},{7,6},{8,9},{9,8},{10,11... | collective-permute-start | bytes 1843208 | tf_op jit(solution)/shard_map/ppermute | solution.py:47
  122.7 54.7 %collective-permute-start.18 = (bf16[40,7680]{1,0:T(8,128)(2,1)S(1)}, bf16[40,7680]{1,0:T(8,128)(2,1)S(1)}, u32[]{:S(2)}, u32[]{:S(2)}) collective-permute-start(bf16[40,7680]{1,0:T(8,128)(2,1)S(1)} %get-tuple-element.22), channel_id=1, source_target_pairs={{0,3},{1,2},{2,1},{3,0},{4,7},{5,6},{6,5},{7,4},{8,11},{9,10},{10,... | collective-permute-start | bytes 1843208 | tf_op jit(solution)/shard_map/ppermute | solution.py:47
  124.8 52.5 %collective-permute-start.17 = (bf16[40,7680]{1,0:T(8,128)(2,1)S(1)}, bf16[40,7680]{1,0:T(8,128)(2,1)S(1)}, u32[]{:S(2)}, u32[]{:S(2)}) collective-permute-start(bf16[40,7680]{1,0:T(8,128)(2,1)S(1)} %get-tuple-element.21), channel_id=1, source_target_pairs={{0,2},{1,3},{2,0},{3,1},{4,6},{5,7},{6,4},{7,5},{8,10},{9,11},{10,... | collective-permute-start | bytes 1843208 | tf_op jit(solution)/shard_map/ppermute | solution.py:47
  149.1 29.8 %copy-start.38 = (s32[4]{0:T(128)S(1)}, s32[4]{0:T(128)}, u32[]{:S(2)}) copy-start(s32[4]{0:T(128)} %param.15) | copy-start | bytes 52
  149.1 30.0 %copy-start.35 = (s32[4,4]{1,0:T(4,128)S(1)}, s32[4,4]{1,0:T(4,128)}, u32[]{:S(2)}) copy-start(s32[4,4]{1,0:T(4,128)} %param.14) | copy-start | bytes 196
  149.2 30.7 %copy-start.2 = (bf16[256,1280]{1,0:T(8,128)(2,1)S(1)}, bf16[256,1280]{1,0:T(8,128)(2,1)}, u32[]{:S(2)}) copy-start(bf16[256,1280]{1,0:T(8,128)(2,1)} %param.13) | copy-start | bytes 1966084
  180.7 13.8 %collective-permute-start = (bf16[256,1280]{1,0:T(8,128)(2,1)S(1)}, bf16[256,1280]{1,0:T(8,128)(2,1)S(1)}, u32[]{:S(2)}, u32[]{:S(2)}) collective-permute-start(bf16[256,1280]{1,0:T(8,128)(2,1)S(1)} %multiply_convert_fusion.3), channel_id=1, source_target_pairs={{0,1},{1,0},{2,3},{3,2},{4,5},{5,4},{6,7},{7,6},{8,9},{9,8},{10,11... | collective-permute-start | bytes 1966088 | tf_op jit(solution)/shard_map/ppermute | solution.py:47
  218.1 14.0 %collective-permute-start.4 = (bf16[256,1280]{1,0:T(8,128)(2,1)S(1)}, bf16[256,1280]{1,0:T(8,128)(2,1)S(1)}, u32[]{:S(2)}, u32[]{:S(2)}) collective-permute-start(bf16[256,1280]{1,0:T(8,128)(2,1)S(1)} %slice.431), channel_id=1, source_target_pairs={{0,1},{1,0},{2,3},{3,2},{4,5},{5,4},{6,7},{7,6},{8,9},{9,8},{10,11... | collective-permute-start | bytes 1966088 | tf_op jit(solution)/shard_map/ppermute | solution.py:47
  232.9 12.1 %collective-permute-start.5 = (bf16[256,1280]{1,0:T(8,128)(2,1)S(1)}, bf16[256,1280]{1,0:T(8,128)(2,1)S(1)}, u32[]{:S(2)}, u32[]{:S(2)}) collective-permute-start(bf16[256,1280]{1,0:T(8,128)(2,1)S(1)} %multiply_convert_fusion.2), channel_id=1, source_target_pairs={{0,1},{1,0},{2,3},{3,2},{4,5},{5,4},{6,7},{7,6},{8,9},{9,8},{10,11... | collective-permute-start | bytes 1966088 | tf_op jit(solution)/shard_map/ppermute | solution.py:47
  245.0 8.8 %copy-start.36 = (bf16[1280,7680]{1,0:T(8,128)(2,1)S(1)}, bf16[1280,7680]{1,0:T(8,128)(2,1)}, u32[]{:S(2)}) copy-start(bf16[1280,7680]{1,0:T(8,128)(2,1)} %all-gather.7.cloned.1.call-done) | copy-start | bytes 58982404
  271.4 13.9 %collective-permute-start.9 = (bf16[256,1280]{1,0:T(8,128)(2,1)S(1)}, bf16[256,1280]{1,0:T(8,128)(2,1)S(1)}, u32[]{:S(2)}, u32[]{:S(2)}) collective-permute-start(bf16[256,1280]{1,0:T(8,128)(2,1)S(1)} %slice.430), channel_id=1, source_target_pairs={{0,1},{1,0},{2,3},{3,2},{4,5},{5,4},{6,7},{7,6},{8,9},{9,8},{10,11... | collective-permute-start | bytes 1966088 | tf_op jit(solution)/shard_map/ppermute | solution.py:47
  286.2 10.7 %collective-permute-start.10 = (bf16[256,1280]{1,0:T(8,128)(2,1)S(1)}, bf16[256,1280]{1,0:T(8,128)(2,1)S(1)}, u32[]{:S(2)}, u32[]{:S(2)}) collective-permute-start(bf16[256,1280]{1,0:T(8,128)(2,1)S(1)} %multiply_convert_fusion.1), channel_id=1, source_target_pairs={{0,1},{1,0},{2,3},{3,2},{4,5},{5,4},{6,7},{7,6},{8,9},{9,8},{10,11... | collective-permute-start | bytes 1966088 | tf_op jit(solution)/shard_map/ppermute | solution.py:47
  321.2 16.0 %collective-permute-start.14 = (bf16[256,1280]{1,0:T(8,128)(2,1)S(1)}, bf16[256,1280]{1,0:T(8,128)(2,1)S(1)}, u32[]{:S(2)}, u32[]{:S(2)}) collective-permute-start(bf16[256,1280]{1,0:T(8,128)(2,1)S(1)} %slice.429), channel_id=1, source_target_pairs={{0,1},{1,0},{2,3},{3,2},{4,5},{5,4},{6,7},{7,6},{8,9},{9,8},{10,11... | collective-permute-start | bytes 1966088 | tf_op jit(solution)/shard_map/ppermute | solution.py:47
  338.1 16.8 %collective-permute-start.15 = (bf16[256,1280]{1,0:T(8,128)(2,1)S(1)}, bf16[256,1280]{1,0:T(8,128)(2,1)S(1)}, u32[]{:S(2)}, u32[]{:S(2)}) collective-permute-start(bf16[256,1280]{1,0:T(8,128)(2,1)S(1)} %multiply_convert_fusion), channel_id=1, source_target_pairs={{0,1},{1,0},{2,3},{3,2},{4,5},{5,4},{6,7},{7,6},{8,9},{9,8},{10,11... | collective-permute-start | bytes 1966088 | tf_op jit(solution)/shard_map/ppermute | solution.py:47
  354.9 8.5 %copy-start.37 = (bf16[1280,7680]{1,0:T(8,128)(2,1)S(1)}, bf16[1280,7680]{1,0:T(8,128)(2,1)}, u32[]{:S(2)}) copy-start(bf16[1280,7680]{1,0:T(8,128)(2,1)} %all-gather.11.cloned.1.call-done) | copy-start | bytes 58982404
  377.5 21.7 %copy-start.1 = (f32[32,1280]{1,0:T(8,128)S(1)}, f32[32,1280]{1,0:T(8,128)}, u32[]{:S(2)}) copy-start(f32[32,1280]{1,0:T(8,128)} %param.16) | copy-start | bytes 491524
  381.2 17.0 %collective-permute-start.19 = (bf16[256,1280]{1,0:T(8,128)(2,1)S(1)}, bf16[256,1280]{1,0:T(8,128)(2,1)S(1)}, u32[]{:S(2)}, u32[]{:S(2)}) collective-permute-start(bf16[256,1280]{1,0:T(8,128)(2,1)S(1)} %slice.428), channel_id=1, source_target_pairs={{0,1},{1,0},{2,3},{3,2},{4,5},{5,4},{6,7},{7,6},{8,9},{9,8},{10,11... | collective-permute-start | bytes 1966088 | tf_op jit(solution)/shard_map/ppermute | solution.py:47
  (15 other events, 52.5 us)
Sparse Core Ops, SparseCore 0:
  40.1 46.7 all-gather.4
  100.9 101.8 all-gather.6
  204.7 46.4 all-gather.8
  252.9 101.9 all-gather.10
